TPU v7x, 32 devices: a whole 2x2x4 slice. The times are simulated.
32 devices in a mesh: rp: 8 (over y, x, core), re: 4 (over z).
Axes of the slice: x: 2, y: 2, z: 4, core: 2. Of those that a mesh axis runs over, the one named last changes fastest.
Arguments:
- coupling: bfloat16 [128, 4, 2, 6, 4096], P('rp', 're'), may hold values from -1.25 to 1.25
- rp_coords: int32 [3, 128], P(None, 'rp'), may hold values from -8 to 8
- degeneracy: int32 [128], P('rp'), may hold values from 1 to 8
- qpoints: int32 [3, 64], replicated, may hold values from 0 to 15
- eigvec: float32 [64, 2, 6, 6], P('rp'), may hold values from -1.75 to 1.75
Outputs:
- coupling_q: float32 [64, 4, 2, 6, 4096], P('rp', None, None, None, 're')
All inputs are finite; a program needn't handle non-finite values.
Results may differ from a plain program's by a relative error of at most 0.0042.
Values may be sent and summed in bfloat16 or wider, within the bound.
A program may use at most 64 MiB of HBM per device.

v0:
```python
import functools
import math

import jax
import jax.numpy as jnp
from jax import lax
from jax.experimental import pallas as pl
from jax.experimental.pallas import tpu as pltpu
from jax.sharding import PartitionSpec as P

QGRID = 16
MESH = pl.DeviceIdType.MESH


def phases(points, coords, degeneracy):
    turns = jnp.mod(points[0][:, None] * coords[0][None, :], QGRID)
    turns = turns + jnp.mod(points[1][:, None] * coords[1][None, :], QGRID)
    turns = turns + jnp.mod(points[2][:, None] * coords[2][None, :], QGRID)
    turns = jnp.mod(turns, QGRID)
    angles = turns.astype(jnp.float32) * (2.0 * math.pi / QGRID)
    weights = 1.0 / degeneracy.astype(jnp.float32)
    table = jnp.concatenate(
        [jnp.cos(angles) * weights[None, :], jnp.sin(angles) * weights[None, :]], axis=0
    )
    return table.astype(jnp.bfloat16)


def combine(table, coupling):
    point_count = table.shape[0] // 2
    product = jnp.dot(
        table, coupling.reshape(coupling.shape[0], -1), preferred_element_type=jnp.float32
    )
    product = product.reshape((2, point_count) + coupling.shape[1:])
    real_part = product[0, :, :, 0] - product[1, :, :, 1]
    imag_part = product[0, :, :, 1] + product[1, :, :, 0]
    return jnp.stack([real_part, imag_part], axis=2)


def mode_mix(values, matrix):
    return jnp.einsum("qrkp,qkn->qrnp", values, matrix, precision=lax.Precision.HIGHEST)


def rotate(summed, eigvec):
    real_in = summed[:, :, 0]
    imag_in = summed[:, :, 1]
    vec_real = eigvec[:, 0]
    vec_imag = eigvec[:, 1]
    real_out = mode_mix(real_in, vec_real) - mode_mix(imag_in, vec_imag)
    imag_out = mode_mix(real_in, vec_imag) + mode_mix(imag_in, vec_real)
    return jnp.stack([real_out, imag_out], axis=2)


def to_owners(all_points):
    return lax.all_to_all(all_points, "rp", split_axis=0, concat_axis=3, tiled=True)


def per_device(coupling, rp_coords, degeneracy, qpoints, eigvec):
    stacked = jnp.concatenate([rp_coords, degeneracy[None, :]], axis=0)
    lattice = lax.all_gather(stacked, "rp", axis=1, tiled=True)
    table = phases(qpoints, lattice[:3], lattice[3])
    rp_count = lax.axis_size("rp")
    re_count = lax.axis_size("re")
    local_rp, local_re, parts, mode_count, pair_count = coupling.shape
    q_local = eigvec.shape[0]
    pair_share = pair_count // re_count
    block_cols = mode_count * pair_share
    inner = block_cols // rp_count
    reordered = coupling.reshape(local_rp, local_re, parts, mode_count, re_count, pair_share)
    reordered = jnp.swapaxes(reordered, 3, 4)
    reordered = reordered.reshape(local_rp, local_re, parts, re_count, rp_count, inner)
    reordered = jnp.swapaxes(reordered, 3, 4)
    reordered = reordered.reshape(local_rp, local_re, parts, rp_count * re_count * inner)
    moved = lax.all_to_all(
        lax.all_to_all(reordered, "rp", split_axis=3, concat_axis=0, tiled=True),
        "re",
        split_axis=3,
        concat_axis=1,
        tiled=True,
    )
    all_points = combine(table, moved)
    summed = to_owners(all_points)
    summed = summed.reshape(q_local, summed.shape[1], parts, mode_count, pair_share)
    return rotate(summed, eigvec)


def column_of(angle):
    return [math.cos(2.0 * math.pi * (step - angle) / QGRID) for step in range(QGRID)]


def pick(turns, values):
    picked = jnp.full(turns.shape, values[0], jnp.float32)
    for step in range(1, QGRID):
        picked = jnp.where(turns == step, jnp.float32(values[step]), picked)
    return picked


def far_first(count):
    return sorted(range(count), key=lambda offset: (-min(offset, count - offset), offset))


def exchange_kernel(
    n,
    planes,
    coupling,
    coords,
    degeneracy,
    eigvec,
    points,
    out,
    gathered,
    all_coords,
    all_degeneracy,
    all_eigvec,
    summed,
    vectors,
    turned,
    outgoing,
    own_sem,
    block_send,
    block_recv,
    first_send,
    first_recv,
    second_send,
    second_recv,
):
    me = lax.axis_index("rp")
    plane = lax.axis_index("re")
    local_rp, modes, parts, pairs = coupling.shape
    share = pairs // planes
    lanes = share // n
    q_local = eigvec.shape[0]
    q_count = n * q_local
    q_rows = q_local * modes * parts
    total_rp = n * local_rp
    offsets = far_first(planes)

    barrier = pltpu.get_barrier_semaphore()

    def greet(index, carry):
        pl.semaphore_signal(
            barrier,
            inc=1,
            device_id={
                "rp": lax.rem(me + lax.rem(index, n), n),
                "re": lax.rem(plane + index // n, planes),
            },
            device_id_type=MESH,
        )
        return carry

    lax.fori_loop(1, n * planes, greet, 0)
    pl.semaphore_wait(barrier, n * planes - 1)

    def peer(shift):
        return lax.rem(me + shift, n)

    def source(shift):
        return lax.rem(me + n - shift, n)

    small = ((coords, all_coords), (degeneracy, all_degeneracy), (eigvec, all_eigvec))

    def block_copies(shift, slot):
        return [
            pltpu.make_async_remote_copy(
                src_ref=held,
                dst_ref=full.at[slot],
                send_sem=block_send.at[shift, index],
                recv_sem=block_recv.at[slot, index],
                device_id={"rp": peer(shift)},
                device_id_type=MESH,
            )
            for index, (held, full) in enumerate(small)
        ]

    def own_blocks():
        return [
            pltpu.make_async_copy(held, full.at[me], own_sem.at[planes * modes + 1 + index])
            for index, (held, full) in enumerate(small)
        ]

    def piece(offset, owner, mode):
        target = lax.rem(plane + offset, planes)
        start = pl.multiple_of(target * share + owner * lanes, lanes)
        return coupling.at[:, mode, :, pl.ds(start, lanes)]

    def landing(offset, slot, mode):
        return gathered.at[offset, mode, pl.ds(slot * local_rp, local_rp)]

    def first_copy(offset, shift, slot, mode):
        return pltpu.make_async_remote_copy(
            src_ref=piece(offset, peer(shift), mode),
            dst_ref=landing(offset, slot, mode),
            send_sem=first_send.at[offset, shift, mode],
            recv_sem=first_recv.at[offset, slot, mode],
            device_id={"rp": peer(shift)},
            device_id_type=MESH,
        )

    def own_copy(offset, mode):
        return pltpu.make_async_copy(
            piece(offset, me, mode), landing(offset, me, mode), own_sem.at[offset * modes + mode]
        )

    def leaving(offset, owner):
        return outgoing.at[offset, pl.ds(owner * q_local, q_local)]

    def home(origin, slot):
        return out.at[:, origin, :, :, pl.ds(pl.multiple_of(slot * lanes, lanes), lanes)]

    def arrival(offset, slot):
        return home(lax.rem(plane + planes - offset, planes), slot)

    def second_copy(offset, shift, slot):
        return pltpu.make_async_remote_copy(
            src_ref=leaving(offset, peer(shift)),
            dst_ref=home(plane, me),
            send_sem=second_send.at[offset, shift],
            recv_sem=second_recv.at[offset, slot],
            device_id={"rp": peer(shift), "re": lax.rem(plane + offset, planes)},
            device_id_type=MESH,
        )

    def second_wait(offset, shift):
        return pltpu.make_async_remote_copy(
            src_ref=leaving(offset, peer(shift)),
            dst_ref=arrival(offset, source(shift)),
            send_sem=second_send.at[offset, shift],
            recv_sem=second_recv.at[offset, source(shift)],
            device_id={"rp": peer(shift), "re": lax.rem(plane + offset, planes)},
            device_id_type=MESH,
        )

    def local_second():
        return pltpu.make_async_copy(
            leaving(0, me), arrival(0, me), own_sem.at[planes * modes]
        )

    def send_first(offset):
        for mode in range(modes):
            for shift in range(1, n):
                first_copy(offset, shift, me, mode).start()
            own_copy(offset, mode).start()

    for shift in range(1, n):
        for copy in block_copies(shift, me):
            copy.start()
    for copy in own_blocks():
        copy.start()
    for offset in offsets[:2]:
        send_first(offset)

    for copy in own_blocks():
        copy.wait()
    for shift in range(1, n):
        for copy in block_copies(shift, source(shift)):
            copy.wait_recv()

    width = parts * total_rp
    repeat = lax.broadcasted_iota(jnp.int32, (total_rp, width), 1) // parts
    repeat = repeat == lax.broadcasted_iota(jnp.int32, (total_rp, width), 0)
    repeat = repeat.astype(jnp.bfloat16)

    def twice(full):
        row = jnp.concatenate([full[slot] for slot in range(n)], axis=1)
        row = row.astype(jnp.float32).astype(jnp.bfloat16)
        return jnp.dot(row, repeat, preferred_element_type=jnp.float32)

    turns = lax.dot_general(
        points[...].astype(jnp.float32).astype(jnp.bfloat16),
        twice(all_coords).astype(jnp.bfloat16),
        (((0,), (0,)), ((), ())),
        preferred_element_type=jnp.float32,
    )
    turns = turns.astype(jnp.int32) & (QGRID - 1)
    weights = 1.0 / twice(all_degeneracy)
    cos = pick(turns, column_of(0.0)) * weights
    sin = pick(turns, column_of(QGRID / 4)) * weights
    real_part = lax.rem(lax.broadcasted_iota(jnp.int32, (q_count, width), 1), parts) == 0
    table = jnp.concatenate(
        [jnp.where(real_part, cos, -sin), jnp.where(real_part, sin, cos)], axis=0
    ).astype(jnp.bfloat16)

    placed = all_eigvec[...].reshape(q_count, parts * modes * modes)
    for entry in range(parts * modes * modes):
        vectors[entry] = jnp.broadcast_to(placed[:, entry : entry + 1], (q_count, lanes))

    for turn, offset in enumerate(offsets):
        for mode in range(modes):
            own_copy(offset, mode).wait()
            for shift in range(1, n):
                first_copy(offset, shift, source(shift), mode).wait_recv()
            summed[:, mode * lanes : (mode + 1) * lanes] = jnp.dot(
                table,
                gathered[offset, mode].reshape(width, lanes),
                preferred_element_type=jnp.float32,
            )

        def rotate_rows(slot, carry):
            start = pl.multiple_of(slot * q_local, q_local)
            rows_at = pl.ds(start, q_local)
            imag_at = pl.ds(q_count + start, q_local)
            real_in = [summed[rows_at, k * lanes : (k + 1) * lanes] for k in range(modes)]
            imag_in = [summed[imag_at, k * lanes : (k + 1) * lanes] for k in range(modes)]
            for mode in range(modes):
                real_out = jnp.zeros((q_local, lanes), jnp.float32)
                imag_out = jnp.zeros((q_local, lanes), jnp.float32)
                for k in range(modes):
                    vec_real = vectors[k * modes + mode, rows_at, :]
                    vec_imag = vectors[(modes + k) * modes + mode, rows_at, :]
                    real_out += real_in[k] * vec_real - imag_in[k] * vec_imag
                    imag_out += real_in[k] * vec_imag + imag_in[k] * vec_real
                first_row = slot * q_rows + mode * parts
                turned[pl.ds(first_row, q_local, stride=modes * parts), :] = real_out
                turned[pl.ds(first_row + 1, q_local, stride=modes * parts), :] = imag_out
            return carry

        lax.fori_loop(0, n, rotate_rows, 0)
        outgoing[offset] = (
            turned[...].astype(jnp.bfloat16).reshape(q_count, modes, parts, lanes)
        )
        for shift in range(n):
            if offset == 0 and shift == 0:
                local_second().start()
            else:
                second_copy(offset, shift, me).start()
        if turn + 2 < planes:
            send_first(offsets[turn + 2])

    for shift in range(1, n):
        for copy in block_copies(shift, me):
            copy.wait_send()
    for offset in offsets:
        for shift in range(n):
            if shift:
                for mode in range(modes):
                    first_copy(offset, shift, me, mode).wait_send()
            if offset == 0 and shift == 0:
                local_second().wait()
            else:
                second_copy(offset, shift, me).wait_send()
                second_wait(offset, shift).wait_recv()


def exchanged(coupling, rp_coords, degeneracy, qpoints, eigvec):
    n = lax.axis_size("rp")
    planes = lax.axis_size("re")
    local_rp, local_re, parts, modes, pairs = coupling.shape
    q_local = eigvec.shape[0]
    lanes = pairs // planes // n
    total_rp = local_rp * n
    q_count = q_local * n
    entries = parts * modes * modes
    gathered = pl.pallas_call(
        functools.partial(exchange_kernel, n, planes),
        out_shape=jax.ShapeDtypeStruct((q_local, planes, modes, parts, n * lanes), jnp.bfloat16),
        in_specs=[
            pl.BlockSpec(memory_space=pl.ANY),
            pl.BlockSpec(memory_space=pl.ANY),
            pl.BlockSpec(memory_space=pl.ANY),
            pl.BlockSpec(memory_space=pl.ANY),
            pl.BlockSpec(memory_space=pltpu.VMEM),
        ],
        out_specs=pl.BlockSpec(memory_space=pl.ANY),
        scratch_shapes=[
            pltpu.VMEM((planes, modes, total_rp, parts, lanes), jnp.bfloat16),
            pltpu.VMEM((n,) + rp_coords.shape, jnp.int32),
            pltpu.VMEM((n, 1, local_rp), jnp.int32),
            pltpu.VMEM((n, q_local, entries), jnp.float32),
            pltpu.VMEM((parts * q_count, modes * lanes), jnp.float32),
            pltpu.VMEM((entries, q_count, lanes), jnp.float32),
            pltpu.VMEM((q_count * modes * parts, lanes), jnp.float32),
            pltpu.VMEM((planes, q_count, modes, parts, lanes), jnp.bfloat16),
            pltpu.SemaphoreType.DMA((planes * modes + 4,)),
            pltpu.SemaphoreType.DMA((n, 3)),
            pltpu.SemaphoreType.DMA((n, 3)),
            pltpu.SemaphoreType.DMA((planes, n, modes)),
            pltpu.SemaphoreType.DMA((planes, n, modes)),
            pltpu.SemaphoreType.DMA((planes, n)),
            pltpu.SemaphoreType.DMA((planes, n)),
        ],
        compiler_params=pltpu.CompilerParams(collective_id=0, has_side_effects=True),
    )(
        jnp.swapaxes(coupling[:, 0], 1, 2),
        rp_coords,
        degeneracy[None, :],
        eigvec.reshape(q_local, entries),
        qpoints,
    )
    return jnp.swapaxes(gathered, 2, 3).astype(jnp.float32)


def fits(n, planes, coupling, eigvec):
    local_rp, local_re, parts, modes, pairs = coupling.shape
    return (
        local_re == 1
        and parts * modes * modes <= local_rp * n == 128
        and pairs // planes // n == 128
        and eigvec.shape[0] == 8
        and modes <= 8
    )


def either(coupling, rp_coords, degeneracy, qpoints, eigvec):
    if fits(lax.axis_size("rp"), lax.axis_size("re"), coupling, eigvec):
        return exchanged(coupling, rp_coords, degeneracy, qpoints, eigvec)
    return per_device(coupling, rp_coords, degeneracy, qpoints, eigvec)


def solution(mesh):
    return jax.shard_map(
        either,
        mesh=mesh,
        in_specs=(
            P("rp", "re", None, None, None),
            P(None, "rp"),
            P("rp"),
            P(),
            P("rp", None, None, None),
        ),
        out_specs=P("rp", None, None, None, "re"),
        check_vma=False,
    )
```

profile of v0, /device:TPU:0, one launch (start us, length us, event | category | flops | bytes accessed | tf_op | source)
XLA Modules:
  0.0 47.0 jit_solution(129150240994441526)
XLA Ops:
  0.0 0.9 %copy.7 = f32[8,2,6,6]{3,2,1,0:T(8,128)S(1)} copy(f32[8,2,6,6]{0,1,3,2:T(2,128)} %param.9) | data formatting | bytes 4608 | tf_op args[4]
  0.9 0.7 %reshape.3.eigvec = f32[8,72]{1,0:T(8,128)} reshape(f32[8,2,6,6]{3,2,1,0:T(8,128)S(1)} %copy.7) | data formatting | bytes 4608 | tf_op jit(solution)/shard_map/reshape | solution.py:386
  1.6 42.3 %shard_map.55 = bf16[8,4,6,2,1024]{4,3,2,1,0:T(2,128)(2,1)} custom-call(bf16[16,6,2,4096]{3,2,1,0:T(2,128)(2,1)} %bitcast.6, s32[3,16]{1,0:T(4,128)} %coords.1, s32[1,16]{1,0:T(1,128)} %bitcast.7, f32[8,72]{1,0:T(8,128)} %reshape.3.eigvec, s32[3,64]{1,0:T(4,128)} %points.1), custom_call_target="tpu_custom_call" | custom-call | tf_op jit(solution)/shard_map/pallas_call | solution.py:353
  43.9 3.1 %convert_bitcast_fusion = f32[8,4,2,6,1024]{4,2,3,1,0:T(2,128)} fusion(bf16[8,4,6,2,1024]{4,3,2,1,0:T(2,128)(2,1)} %shard_map.55), kind=kLoop, calls=%fused_computation | loop fusion | flops 393216 | bytes 2359296 | tf_op jit(solution)/shard_map/convert_element_type | solution.py:389
where the time goes:
time: 47.3 us; the launch traced here: 47 us
  Pallas kernels  42.3 us (89%)
  other arithmetic  3.12 us (7%)
  local copies, waits for them, and re-layouts  1.59 us (3%)
    pallas_call x1, Pallas kernels, exchanged(): pl.pallas_call(functools.partial(exchange_kernel, n, planes), out_shape=j...  42.3 us
    convert_element_type x1, other arithmetic, exchanged(): return jnp.swapaxes(gathered, 2, 3).astype(jnp.float32)  3.12 us

commit v1 on v0

v1 whole, which is shorter than its diff:
```python
import functools
import math

import jax
import jax.numpy as jnp
from jax import lax
from jax.experimental import pallas as pl
from jax.experimental.pallas import tpu as pltpu
from jax.sharding import PartitionSpec as P

QGRID = 16
MESH = pl.DeviceIdType.MESH


def phases(points, coords, degeneracy):
    turns = jnp.mod(points[0][:, None] * coords[0][None, :], QGRID)
    turns = turns + jnp.mod(points[1][:, None] * coords[1][None, :], QGRID)
    turns = turns + jnp.mod(points[2][:, None] * coords[2][None, :], QGRID)
    turns = jnp.mod(turns, QGRID)
    angles = turns.astype(jnp.float32) * (2.0 * math.pi / QGRID)
    weights = 1.0 / degeneracy.astype(jnp.float32)
    table = jnp.concatenate(
        [jnp.cos(angles) * weights[None, :], jnp.sin(angles) * weights[None, :]], axis=0
    )
    return table.astype(jnp.bfloat16)


def combine(table, coupling):
    point_count = table.shape[0] // 2
    product = jnp.dot(
        table, coupling.reshape(coupling.shape[0], -1), preferred_element_type=jnp.float32
    )
    product = product.reshape((2, point_count) + coupling.shape[1:])
    real_part = product[0, :, :, 0] - product[1, :, :, 1]
    imag_part = product[0, :, :, 1] + product[1, :, :, 0]
    return jnp.stack([real_part, imag_part], axis=2)


def mode_mix(values, matrix):
    return jnp.einsum("qrkp,qkn->qrnp", values, matrix, precision=lax.Precision.HIGHEST)


def rotate(summed, eigvec):
    real_in = summed[:, :, 0]
    imag_in = summed[:, :, 1]
    vec_real = eigvec[:, 0]
    vec_imag = eigvec[:, 1]
    real_out = mode_mix(real_in, vec_real) - mode_mix(imag_in, vec_imag)
    imag_out = mode_mix(real_in, vec_imag) + mode_mix(imag_in, vec_real)
    return jnp.stack([real_out, imag_out], axis=2)


def to_owners(all_points):
    return lax.all_to_all(all_points, "rp", split_axis=0, concat_axis=3, tiled=True)


def per_device(coupling, rp_coords, degeneracy, qpoints, eigvec):
    stacked = jnp.concatenate([rp_coords, degeneracy[None, :]], axis=0)
    lattice = lax.all_gather(stacked, "rp", axis=1, tiled=True)
    table = phases(qpoints, lattice[:3], lattice[3])
    rp_count = lax.axis_size("rp")
    re_count = lax.axis_size("re")
    local_rp, local_re, parts, mode_count, pair_count = coupling.shape
    q_local = eigvec.shape[0]
    pair_share = pair_count // re_count
    block_cols = mode_count * pair_share
    inner = block_cols // rp_count
    reordered = coupling.reshape(local_rp, local_re, parts, mode_count, re_count, pair_share)
    reordered = jnp.swapaxes(reordered, 3, 4)
    reordered = reordered.reshape(local_rp, local_re, parts, re_count, rp_count, inner)
    reordered = jnp.swapaxes(reordered, 3, 4)
    reordered = reordered.reshape(local_rp, local_re, parts, rp_count * re_count * inner)
    moved = lax.all_to_all(
        lax.all_to_all(reordered, "rp", split_axis=3, concat_axis=0, tiled=True),
        "re",
        split_axis=3,
        concat_axis=1,
        tiled=True,
    )
    all_points = combine(table, moved)
    summed = to_owners(all_points)
    summed = summed.reshape(q_local, summed.shape[1], parts, mode_count, pair_share)
    return rotate(summed, eigvec)


def column_of(angle):
    return [math.cos(2.0 * math.pi * (step - angle) / QGRID) for step in range(QGRID)]


def pick(turns, values):
    picked = jnp.full(turns.shape, values[0], jnp.float32)
    for step in range(1, QGRID):
        picked = jnp.where(turns == step, jnp.float32(values[step]), picked)
    return picked


def flip(index, bits):
    for bit in (1, 2, 4):
        if bits & bit:
            index = index + bit - 2 * bit * (index // bit % 2)
    return index


def place(index, gather):
    return 2 * (index // gather % 2) + index % 2


def rotation_kernel(
    n,
    planes,
    coupling,
    coords,
    degeneracy,
    eigvec,
    points,
    out,
    gathered,
    all_coords,
    all_degeneracy,
    all_eigvec,
    table_rows,
    vectors,
    kept,
    leaving,
    arriving,
    turned,
    own_sem,
    small_send,
    small_recv,
    first_send,
    first_recv,
    middle_send,
    middle_recv,
    last_send,
    last_recv,
):
    me = lax.axis_index("rp")
    plane = lax.axis_index("re")
    local_rp, modes, parts, pairs = coupling.shape
    lanes = gathered.shape[-1]
    q_local = eigvec.shape[-1]
    group = 4
    tile = parts * q_local
    half = group * tile
    width = group * local_rp * parts
    steps = (2, 3, 1, 0)
    sets = ((0, 4, 2), (1, 2, 4))
    near = (0, 1, 4, 5, 2, 3)

    barrier = pltpu.get_barrier_semaphore()

    def greet(bits, step):
        pl.semaphore_signal(
            barrier,
            inc=1,
            device_id={"rp": flip(me, bits), "re": flip(plane, step)},
            device_id_type=MESH,
        )

    for step in steps:
        for bits in near:
            if bits or step:
                greet(bits, step)
    pl.semaphore_wait(barrier, len(near) * planes - 1)

    def local(source, target, index):
        return pltpu.make_async_copy(source, target, own_sem.at[index])

    def remote(source, target, send, recv, bits, step=0):
        return pltpu.make_async_remote_copy(
            src_ref=source,
            dst_ref=target,
            send_sem=send,
            recv_sem=recv,
            device_id={"rp": flip(me, bits), "re": flip(plane, step)},
            device_id_type=MESH,
        )

    def members(gather):
        return (gather + 1, gather, 1)

    def small_copies(sender):
        copies = []
        for index, gather, _ in sets:
            for turn, bits in enumerate(members(gather)):
                slot = place(me if sender else flip(me, bits), gather)
                at = index * 3 + turn
                for kind, (held, full) in enumerate(
                    ((coords, all_coords), (degeneracy, all_degeneracy))
                ):
                    copies.append(
                        remote(
                            held,
                            full.at[index, slot],
                            small_send.at[kind, at],
                            small_recv.at[kind, at],
                            bits,
                        )
                    )
        for turn, bits in enumerate(near):
            if bits:
                copies.append(
                    remote(
                        eigvec,
                        all_eigvec.at[turn],
                        small_send.at[2, turn],
                        small_recv.at[2, turn],
                        bits,
                    )
                )
        return copies

    def small_own():
        copies = []
        for index, gather, _ in sets:
            slot = place(me, gather)
            copies.append(local(coords, all_coords.at[index, slot], 2 * index))
            copies.append(local(degeneracy, all_degeneracy.at[index, slot], 2 * index + 1))
        copies.append(local(eigvec, all_eigvec.at[0], 4))
        return copies

    def piece(step, index, owner, gather):
        block = (flip(plane, step) * 2 + index) * group + place(owner, gather)
        return coupling.at[:, :, :, pl.ds(pl.multiple_of(block * lanes, lanes), lanes)]

    def landing(step, index, origin, gather):
        return gathered.at[step, index, pl.ds(place(origin, gather) * local_rp, local_rp)]

    def first_copy(step, index, gather, turn, bits, sender):
        origin = me if sender else flip(me, bits)
        return remote(
            piece(step, index, flip(me, bits), gather),
            landing(step, index, origin, gather),
            first_send.at[step, index, turn],
            first_recv.at[step, index, turn],
            bits,
        )

    def first_own(step, index, gather):
        return local(
            piece(step, index, me, gather),
            landing(step, index, me, gather),
            5 + 2 * step + index,
        )

    def send_first(step):
        for turn in range(3):
            for index, gather, _ in sets:
                first_copy(step, index, gather, turn, members(gather)[turn], True).start()
        for index, gather, _ in sets:
            first_own(step, index, gather).start()

    def middle_copy(step, index, other):
        return remote(
            leaving.at[step, index],
            arriving.at[step, index],
            middle_send.at[step, index],
            middle_recv.at[step, index],
            other,
        )

    def final_block(index, origin, gather):
        return index * group + place(origin, gather)

    def last_copy(step, index, gather, turn, bits, sender):
        origin = me if sender else flip(me, bits)
        home = plane if sender else flip(plane, step)
        source = turned.at[step, index, turn]
        target = out.at[home, final_block(index, origin, gather)]
        if not bits and not step:
            return local(source, target, 13 + index)
        return remote(
            source,
            target,
            last_send.at[step, index, turn],
            last_recv.at[step, index, turn],
            bits,
            step,
        )

    for copy in small_copies(True) + small_own():
        copy.start()
    for step in steps[:2]:
        send_first(step)
    for copy in small_own():
        copy.wait()
    for copy in small_copies(False):
        copy.wait_recv()

    columns = lax.broadcasted_iota(jnp.int32, (group * local_rp, width), 1)
    repeat = columns // parts == lax.broadcasted_iota(jnp.int32, (group * local_rp, width), 0)
    repeat = repeat.astype(jnp.bfloat16)

    def twice(full, index):
        row = jnp.concatenate([full[index, slot] for slot in range(group)], axis=1)
        row = row.astype(jnp.float32).astype(jnp.bfloat16)
        return jnp.dot(row, repeat, preferred_element_type=jnp.float32)

    q_count = n * q_local
    real_part = lax.broadcasted_iota(jnp.int32, (q_count, width), 1) % parts == 0
    tables = []
    for index, gather, other in sets:
        turns = lax.dot_general(
            points[...].astype(jnp.float32).astype(jnp.bfloat16),
            twice(all_coords, index).astype(jnp.bfloat16),
            (((0,), (0,)), ((), ())),
            preferred_element_type=jnp.float32,
        )
        turns = turns.astype(jnp.int32) & (QGRID - 1)
        weights = 1.0 / twice(all_degeneracy, index)
        cos = pick(turns, column_of(0.0)) * weights
        sin = pick(turns, column_of(QGRID / 4)) * weights
        to_real = jnp.where(real_part, cos, -sin)
        to_imag = jnp.where(real_part, sin, cos)
        mine = me // other % 2
        for owner in range(n):
            side = owner // other % 2
            apart = side + mine - 2 * side * mine
            row = pl.multiple_of((1 - apart) * half + place(owner, gather) * tile, tile)
            rows = slice(owner * q_local, (owner + 1) * q_local)
            table_rows[index, pl.ds(row, q_local), :] = to_real[rows]
            table_rows[index, pl.ds(row + q_local, q_local), :] = to_imag[rows]

    for turn in range(len(near)):
        flat = all_eigvec[turn].reshape(modes * modes * parts, q_local).T
        for entry in range(modes * modes * parts):
            vectors[turn, entry] = jnp.broadcast_to(flat[:, entry : entry + 1], (q_local, lanes))

    def gather_step(step):
        for index, gather, other in sets:
            first_own(step, index, gather).wait()
            for turn, bits in enumerate(members(gather)):
                first_copy(step, index, gather, turn, bits, False).wait_recv()
            table = table_rows[index].astype(jnp.bfloat16)
            for mode in range(modes):
                product = jnp.dot(
                    table,
                    gathered[step, index, :, mode].reshape(width, lanes),
                    preferred_element_type=jnp.float32,
                )
                at = slice(mode * lanes, (mode + 1) * lanes)
                leaving[step, index, :, at] = product[:half].astype(jnp.bfloat16)
                kept[step, index, :, at] = product[half:]
            middle_copy(step, index, other).start()

    def rotate_step(step):
        for index, gather, other in sets:
            middle_copy(step, index, other).wait_recv()
            for turn, bits in enumerate(members(gather) + (0,)):
                owner = near.index(bits)
                start = pl.multiple_of(place(flip(me, bits), gather) * tile, tile)
                rows = pl.ds(start, tile)
                real_in = []
                imag_in = []
                for k in range(modes):
                    at = slice(k * lanes, (k + 1) * lanes)
                    total = kept[step, index, rows, at] + arriving[
                        step, index, rows, at
                    ].astype(jnp.float32)
                    real_in.append(total[:q_local])
                    imag_in.append(total[q_local:])
                for mode in range(modes):
                    real_out = jnp.zeros((q_local, lanes), jnp.float32)
                    imag_out = jnp.zeros((q_local, lanes), jnp.float32)
                    for k in range(modes):
                        vec_real = vectors[owner, (k * modes + mode) * parts]
                        vec_imag = vectors[owner, (k * modes + mode) * parts + 1]
                        real_out += real_in[k] * vec_real - imag_in[k] * vec_imag
                        imag_out += real_in[k] * vec_imag + imag_in[k] * vec_real
                    turned[step, index, turn, mode] = jnp.concatenate(
                        [real_out, imag_out], axis=0
                    ).astype(jnp.bfloat16)
                last_copy(step, index, gather, turn, bits, True).start()

    gather_step(steps[0])
    send_first(steps[2])
    gather_step(steps[1])
    rotate_step(steps[0])
    send_first(steps[3])
    gather_step(steps[2])
    rotate_step(steps[1])
    gather_step(steps[3])
    rotate_step(steps[2])
    rotate_step(steps[3])

    for copy in small_copies(True):
        copy.wait_send()
    for step in steps:
        for index, gather, other in sets:
            for turn, bits in enumerate(members(gather)):
                first_copy(step, index, gather, turn, bits, True).wait_send()
            middle_copy(step, index, other).wait_send()
            for turn, bits in enumerate(members(gather) + (0,)):
                if bits or step:
                    last_copy(step, index, gather, turn, bits, True).wait_send()
                    last_copy(step, index, gather, turn, bits, False).wait_recv()
                else:
                    last_copy(step, index, gather, turn, bits, True).wait()


def spread_kernel(held, out, rows_of, sems):
    planes, blocks, modes, tile, lanes = held.shape
    q_local = tile // 2
    per_plane = modes * blocks * 2
    per_q = planes * per_plane

    def copies(source):
        return [
            pltpu.make_async_copy(
                rows_of.at[pl.ds(q * per_q + source * per_plane, per_plane)],
                out.at[pl.ds(q * per_q + source * per_plane, per_plane)],
                sems.at[source, q],
            )
            for q in range(q_local)
        ]

    for source in range(planes):
        for mode in range(modes):
            for block in range(blocks):
                values = held[source, block, mode].astype(jnp.float32)
                row = source * per_plane + (mode * blocks + block) * 2
                rows_of[pl.ds(row, q_local, stride=per_q), :] = values[:q_local]
                rows_of[pl.ds(row + 1, q_local, stride=per_q), :] = values[q_local:]
        for copy in copies(source):
            copy.start()
    for source in range(planes):
        for copy in copies(source):
            copy.wait()


def exchanged(coupling, rp_coords, degeneracy, qpoints, eigvec):
    n = lax.axis_size("rp")
    planes = lax.axis_size("re")
    local_rp, local_re, parts, modes, pairs = coupling.shape
    q_local = eigvec.shape[0]
    lanes = pairs // planes // n
    group = n // 2
    tile = parts * q_local
    half = group * tile
    width = group * local_rp * parts
    entries = parts * modes * modes
    near = 6
    gathered = pl.pallas_call(
        functools.partial(rotation_kernel, n, planes),
        out_shape=jax.ShapeDtypeStruct((planes, n, modes, tile, lanes), jnp.bfloat16),
        in_specs=[
            pl.BlockSpec(memory_space=pltpu.HBM),
            pl.BlockSpec(memory_space=pltpu.HBM),
            pl.BlockSpec(memory_space=pltpu.HBM),
            pl.BlockSpec(memory_space=pltpu.HBM),
            pl.BlockSpec(memory_space=pltpu.VMEM),
        ],
        out_specs=pl.BlockSpec(memory_space=pl.ANY),
        scratch_shapes=[
            pltpu.VMEM((planes, 2, group * local_rp, modes, parts, lanes), jnp.bfloat16),
            pltpu.VMEM((2, group) + rp_coords.shape, jnp.int32),
            pltpu.VMEM((2, group, 1, local_rp), jnp.int32),
            pltpu.VMEM((near, modes * modes, parts, q_local), jnp.float32),
            pltpu.VMEM((2, 2 * half, width), jnp.float32),
            pltpu.VMEM((near, entries, q_local, lanes), jnp.float32),
            pltpu.VMEM((planes, 2, half, modes * lanes), jnp.float32),
            pltpu.VMEM((planes, 2, half, modes * lanes), jnp.bfloat16),
            pltpu.VMEM((planes, 2, half, modes * lanes), jnp.bfloat16),
            pltpu.VMEM((planes, 2, group, modes, tile, lanes), jnp.bfloat16),
            pltpu.SemaphoreType.DMA((15,)),
            pltpu.SemaphoreType.DMA((3, near)),
            pltpu.SemaphoreType.DMA((3, near)),
            pltpu.SemaphoreType.DMA((planes, 2, group - 1)),
            pltpu.SemaphoreType.DMA((planes, 2, group - 1)),
            pltpu.SemaphoreType.DMA((planes, 2)),
            pltpu.SemaphoreType.DMA((planes, 2)),
            pltpu.SemaphoreType.DMA((planes, 2, group)),
            pltpu.SemaphoreType.DMA((planes, 2, group)),
        ],
        compiler_params=pltpu.CompilerParams(
            collective_id=0, has_side_effects=True, vmem_limit_bytes=24 * 2**20
        ),
    )(
        jnp.swapaxes(coupling[:, 0], 1, 2),
        rp_coords,
        degeneracy[None, :],
        jnp.transpose(eigvec, (2, 3, 1, 0)).reshape(modes * modes, parts, q_local),
        qpoints,
    )
    rows = q_local * planes * modes * n * parts
    spread = pl.pallas_call(
        spread_kernel,
        out_shape=jax.ShapeDtypeStruct((rows, lanes), jnp.float32),
        in_specs=[pl.BlockSpec(memory_space=pltpu.VMEM)],
        out_specs=pl.BlockSpec(memory_space=pl.ANY),
        scratch_shapes=[
            pltpu.VMEM((rows, lanes), jnp.float32),
            pltpu.SemaphoreType.DMA((planes, q_local)),
        ],
        compiler_params=pltpu.CompilerParams(vmem_limit_bytes=24 * 2**20),
    )(gathered)
    spread = spread.reshape(q_local, planes, modes, n, parts, lanes)
    spread = jnp.transpose(spread, (0, 1, 4, 2, 3, 5))
    return spread.reshape(q_local, planes, parts, modes, n * lanes)


def fits(n, planes, coupling, eigvec):
    local_rp, local_re, parts, modes, pairs = coupling.shape
    return (
        local_re == 1
        and n == 8
        and planes == 4
        and local_rp * n == 128
        and parts * modes * modes <= 128
        and pairs // planes // n == 128
        and eigvec.shape[0] == 8
        and modes <= 8
    )


def either(coupling, rp_coords, degeneracy, qpoints, eigvec):
    if fits(lax.axis_size("rp"), lax.axis_size("re"), coupling, eigvec):
        return exchanged(coupling, rp_coords, degeneracy, qpoints, eigvec)
    return per_device(coupling, rp_coords, degeneracy, qpoints, eigvec)


def solution(mesh):
    return jax.shard_map(
        either,
        mesh=mesh,
        in_specs=(
            P("rp", "re", None, None, None),
            P(None, "rp"),
            P("rp"),
            P(),
            P("rp", None, None, None),
        ),
        out_specs=P("rp", None, None, None, "re"),
        check_vma=False,
    )
```

time: 47.3 us -> 42.2 us (0.89)
  Pallas kernels: 42.3 us -> 37.7 us
  other arithmetic: 3.12 us -> 0 us
  local copies, waits for them, and re-layouts: 1.59 us -> 4.19 us
    pallas_call x1 -> x2, Pallas kernels: 42.3 us -> 37.7 us  [the longest x1 35.8 us: exchanged(): pl.pallas_call(functools.partial(rotation_kernel, n, planes), out_shape=j...]
    unnamed x1 -> x10, local copies, waits for them, and re-layouts: 0.91 us -> 4.19 us
    convert_element_type x1 -> x0, other arithmetic: 3.12 us -> none  [exchanged(): return jnp.swapaxes(gathered, 2, 3).astype(jnp.float32)]
    reshape x1 -> x0, local copies, waits for them, and re-layouts: 0.68 us -> none  [exchanged(): eigvec.reshape(q_local, entries)]
where the time goes in v1:
time: 42.2 us; the launch traced here: 41.9 us
  Pallas kernels  37.7 us (89%)
  local copies, waits for them, and re-layouts  4.19 us (10%)
    pallas_call x1, Pallas kernels, exchanged(): pl.pallas_call(functools.partial(rotation_kernel, n, planes), out_shape=j...  35.8 us
    unnamed x10, local copies, waits for them, and re-layouts  4.19 us
    pallas_call x1, Pallas kernels, exchanged(): pl.pallas_call(spread_kernel, out_shape=jax.ShapeDtypeStruct((rows, lanes...  1.94 us

profile of v1, /device:TPU:0, one launch (start us, length us, event | category | flops | bytes accessed | tf_op | source)
XLA Modules:
  0.0 41.9 jit_solution(11038666917038546014)
XLA Ops:
  0.0 0.0 copy-start
  0.0 1.4 %copy-done = bf16[16,1,2,6,4096]{4,2,3,1,0:T(2,128)(2,1)S(1)} copy-done((bf16[16,1,2,6,4096]{4,2,3,1,0:T(2,128)(2,1)S(1)}, bf16[16,1,2,6,4096]{4,2,3,1,0:T(2,128)(2,1)}, u32[]{:S(2)}) %copy-start) | copy-done | bytes 1572888
  1.4 0.0 copy-start.1
  1.4 0.8 %copy-done.1 = f32[8,2,6,6]{0,1,3,2:T(2,128)S(1)} copy-done((f32[8,2,6,6]{0,1,3,2:T(2,128)S(1)}, f32[8,2,6,6]{0,1,3,2:T(2,128)}, u32[]{:S(2)}) %copy-start.1) | copy-done | bytes 2328
  2.2 0.0 copy-start.2
  2.2 0.7 %copy-done.2 = s32[3,16]{1,0:T(4,128)S(1)} copy-done((s32[3,16]{1,0:T(4,128)S(1)}, s32[3,16]{1,0:T(4,128)}, u32[]{:S(2)}) %copy-start.2) | copy-done | bytes 216
  2.9 0.0 copy-start.3
  2.9 0.7 %copy-done.3 = s32[3,64]{1,0:T(4,128)S(1)} copy-done((s32[3,64]{1,0:T(4,128)S(1)}, s32[3,64]{1,0:T(4,128)}, u32[]{:S(2)}) %copy-start.3) | copy-done | bytes 792
  3.5 0.0 copy-start.4
  3.5 0.7 %copy-done.4 = s32[16]{0:T(128)S(1)} copy-done((s32[16]{0:T(128)S(1)}, s32[16]{0:T(128)}, u32[]{:S(2)}) %copy-start.4) | copy-done | bytes 88
  4.2 35.8 %shard_map.55.held = bf16[4,8,6,16,128]{4,3,2,1,0:T(8,128)(2,1)S(1)} custom-call(bf16[16,6,2,4096]{3,2,1,0:T(2,128)(2,1)S(1)} %bitcast.12, s32[3,16]{1,0:T(4,128)S(1)} %copy-done.2, s32[1,16]{1,0:T(1,128)S(1)} %bitcast.14, f32[36,2,8]{2,1,0:T(2,128)S(1)} %bitcast.13, s32[3,64]{1,0:T(4,128)S(1)} %copy-done.3), custom_call_target="tpu_custom_call" | custom-call | tf_op jit(solution)/shard_map/pallas_call | solution.py:443
  40.0 1.9 %shard_map.56 = f32[3072,128]{1,0:T(8,128)} custom-call(bf16[4,8,6,16,128]{4,3,2,1,0:T(8,128)(2,1)S(1)} %shard_map.55.held), custom_call_target="tpu_custom_call" | custom-call | tf_op jit(solution)/shard_map/pallas_call | solution.py:486
Async XLA Ops:
  0.0 1.4 %copy-start = (bf16[16,1,2,6,4096]{4,2,3,1,0:T(2,128)(2,1)S(1)}, bf16[16,1,2,6,4096]{4,2,3,1,0:T(2,128)(2,1)}, u32[]{:S(2)}) copy-start(bf16[16,1,2,6,4096]{4,2,3,1,0:T(2,128)(2,1)} %param.5) | copy-start | bytes 4718596
  1.4 0.8 %copy-start.1 = (f32[8,2,6,6]{0,1,3,2:T(2,128)S(1)}, f32[8,2,6,6]{0,1,3,2:T(2,128)}, u32[]{:S(2)}) copy-start(f32[8,2,6,6]{0,1,3,2:T(2,128)} %param.9) | copy-start | bytes 6916
  2.2 0.7 %copy-start.2 = (s32[3,16]{1,0:T(4,128)S(1)}, s32[3,16]{1,0:T(4,128)}, u32[]{:S(2)}) copy-start(s32[3,16]{1,0:T(4,128)} %coords.1) | copy-start | bytes 580
  2.9 0.7 %copy-start.3 = (s32[3,64]{1,0:T(4,128)S(1)}, s32[3,64]{1,0:T(4,128)}, u32[]{:S(2)}) copy-start(s32[3,64]{1,0:T(4,128)} %points.1) | copy-start | bytes 2308
  3.5 0.7 %copy-start.4 = (s32[16]{0:T(128)S(1)}, s32[16]{0:T(128)}, u32[]{:S(2)}) copy-start(s32[16]{0:T(128)} %param.7) | copy-start | bytes 196

commit v2 on v1

--- a/solution.py
+++ b/solution.py
@@ -112,8 +112,9 @@
     coords,
     degeneracy,
     eigvec,
+    points_in,
+    out,
     points,
-    out,
     gathered,
     all_coords,
     all_degeneracy,
@@ -133,6 +134,7 @@
     middle_recv,
     last_send,
     last_recv,
+    above_sem,
 ):
     me = lax.axis_index("rp")
     plane = lax.axis_index("re")
@@ -149,19 +151,29 @@
 
     barrier = pltpu.get_barrier_semaphore()
 
-    def greet(bits, step):
+    def greet(semaphore, bits, level):
         pl.semaphore_signal(
-            barrier,
+            semaphore,
             inc=1,
-            device_id={"rp": flip(me, bits), "re": flip(plane, step)},
+            device_id={"rp": flip(me, bits), "re": level},
             device_id_type=MESH,
         )
 
-    for step in steps:
-        for bits in near:
-            if bits or step:
-                greet(bits, step)
-    pl.semaphore_wait(barrier, len(near) * planes - 1)
+    for bits in near[1:]:
+        greet(barrier, bits, plane)
+    for ahead in range(1, planes):
+
+        @pl.when(plane + ahead < planes)
+        def _():
+            for bits in near:
+                greet(barrier, bits, plane + ahead)
+
+    pl.semaphore_wait(barrier, len(near) - 1 + len(near) * plane)
+    for behind in range(1, planes):
+
+        @pl.when(plane >= behind)
+        def _():
+            greet(above_sem, 0, plane - behind)
 
     def local(source, target, index):
         return pltpu.make_async_copy(source, target, own_sem.at[index])
@@ -217,6 +229,7 @@
             copies.append(local(coords, all_coords.at[index, slot], 2 * index))
             copies.append(local(degeneracy, all_degeneracy.at[index, slot], 2 * index + 1))
         copies.append(local(eigvec, all_eigvec.at[0], 4))
+        copies.append(local(points_in, points, 15))
         return copies
 
     def piece(step, index, owner, gather):
@@ -375,6 +388,11 @@
     gather_step(steps[0])
     send_first(steps[2])
     gather_step(steps[1])
+
+    @pl.when(plane < planes - 1)
+    def _():
+        pl.semaphore_wait(above_sem, planes - 1 - plane)
+
     rotate_step(steps[0])
     send_first(steps[3])
     gather_step(steps[2])
@@ -426,6 +444,10 @@
     for source in range(planes):
         for copy in copies(source):
             copy.wait()
+
+
+def in_hbm(value):
+    return pltpu.with_memory_space_constraint(value, pltpu.HBM)
 
 
 def exchanged(coupling, rp_coords, degeneracy, qpoints, eigvec):
@@ -448,10 +470,11 @@
             pl.BlockSpec(memory_space=pltpu.HBM),
             pl.BlockSpec(memory_space=pltpu.HBM),
             pl.BlockSpec(memory_space=pltpu.HBM),
-            pl.BlockSpec(memory_space=pltpu.VMEM),
+            pl.BlockSpec(memory_space=pltpu.HBM),
         ],
         out_specs=pl.BlockSpec(memory_space=pl.ANY),
         scratch_shapes=[
+            pltpu.VMEM(qpoints.shape, jnp.int32),
             pltpu.VMEM((planes, 2, group * local_rp, modes, parts, lanes), jnp.bfloat16),
             pltpu.VMEM((2, group) + rp_coords.shape, jnp.int32),
             pltpu.VMEM((2, group, 1, local_rp), jnp.int32),
@@ -462,7 +485,7 @@
             pltpu.VMEM((planes, 2, half, modes * lanes), jnp.bfloat16),
             pltpu.VMEM((planes, 2, half, modes * lanes), jnp.bfloat16),
             pltpu.VMEM((planes, 2, group, modes, tile, lanes), jnp.bfloat16),
-            pltpu.SemaphoreType.DMA((15,)),
+            pltpu.SemaphoreType.DMA((16,)),
             pltpu.SemaphoreType.DMA((3, near)),
             pltpu.SemaphoreType.DMA((3, near)),
             pltpu.SemaphoreType.DMA((planes, 2, group - 1)),
@@ -471,16 +494,17 @@
             pltpu.SemaphoreType.DMA((planes, 2)),
             pltpu.SemaphoreType.DMA((planes, 2, group)),
             pltpu.SemaphoreType.DMA((planes, 2, group)),
+            pltpu.SemaphoreType.REGULAR,
         ],
         compiler_params=pltpu.CompilerParams(
             collective_id=0, has_side_effects=True, vmem_limit_bytes=24 * 2**20
         ),
     )(
-        jnp.swapaxes(coupling[:, 0], 1, 2),
-        rp_coords,
-        degeneracy[None, :],
-        jnp.transpose(eigvec, (2, 3, 1, 0)).reshape(modes * modes, parts, q_local),
-        qpoints,
+        in_hbm(jnp.swapaxes(coupling[:, 0], 1, 2)),
+        in_hbm(rp_coords),
+        in_hbm(degeneracy[None, :]),
+        in_hbm(jnp.transpose(eigvec, (2, 3, 1, 0)).reshape(modes * modes, parts, q_local)),
+        in_hbm(qpoints),
     )
     rows = q_local * planes * modes * n * parts
     spread = pl.pallas_call(

time: 42.2 us -> 37.3 us (0.88)
  local copies, waits for them, and re-layouts: 4.19 us -> 0 us
  Pallas kernels: 37.7 us -> 37.1 us
    unnamed x10 -> x0, local copies, waits for them, and re-layouts: 4.19 us -> none
    pallas_call x1, Pallas kernels: 35.8 us -> 35.2 us  [exchanged(): pl.pallas_call(functools.partial(rotation_kernel, n, planes), out_shape=j...]
where the time goes in v2:
time: 37.3 us; the launch traced here: 37.1 us
  Pallas kernels  37.1 us (99%)
    pallas_call x1, Pallas kernels, exchanged(): pl.pallas_call(functools.partial(rotation_kernel, n, planes), out_shape=j...  35.2 us
    pallas_call x1, Pallas kernels, exchanged(): pl.pallas_call(spread_kernel, out_shape=jax.ShapeDtypeStruct((rows, lanes...  1.94 us

profile of v2, /device:TPU:0, one launch (start us, length us, event | category | flops | bytes accessed | tf_op | source)
XLA Modules:
  0.0 37.1 jit_solution(15319269455675118449)
XLA Ops:
  0.0 35.2 %shard_map.55.held = bf16[4,8,6,16,128]{4,3,2,1,0:T(8,128)(2,1)S(1)} custom-call(bf16[16,6,2,4096]{3,2,1,0:T(2,128)(2,1)} %bitcast.12, s32[3,16]{1,0:T(4,128)} %coords.1, s32[1,16]{1,0:T(1,128)} %bitcast.14, f32[36,2,8]{2,1,0:T(2,128)} %bitcast.13, s32[3,64]{1,0:T(4,128)} %points_in.1), custom_call_target="tpu_custom_call" | custom-call | tf_op jit(solution)/shard_map/pallas_call | solution.py:465
  35.2 1.9 %shard_map.56 = f32[3072,128]{1,0:T(8,128)} custom-call(bf16[4,8,6,16,128]{4,3,2,1,0:T(8,128)(2,1)S(1)} %shard_map.55.held), custom_call_target="tpu_custom_call" | custom-call | tf_op jit(solution)/shard_map/pallas_call | solution.py:510

commit v3 on v2

v3 whole, which is shorter than its diff:
```python
import functools
import math

import jax
import jax.numpy as jnp
from jax import lax
from jax.experimental import pallas as pl
from jax.experimental.pallas import tpu as pltpu
from jax.sharding import PartitionSpec as P

QGRID = 16
MESH = pl.DeviceIdType.MESH


def phases(points, coords, degeneracy):
    turns = jnp.mod(points[0][:, None] * coords[0][None, :], QGRID)
    turns = turns + jnp.mod(points[1][:, None] * coords[1][None, :], QGRID)
    turns = turns + jnp.mod(points[2][:, None] * coords[2][None, :], QGRID)
    turns = jnp.mod(turns, QGRID)
    angles = turns.astype(jnp.float32) * (2.0 * math.pi / QGRID)
    weights = 1.0 / degeneracy.astype(jnp.float32)
    table = jnp.concatenate(
        [jnp.cos(angles) * weights[None, :], jnp.sin(angles) * weights[None, :]], axis=0
    )
    return table.astype(jnp.bfloat16)


def combine(table, coupling):
    point_count = table.shape[0] // 2
    product = jnp.dot(
        table, coupling.reshape(coupling.shape[0], -1), preferred_element_type=jnp.float32
    )
    product = product.reshape((2, point_count) + coupling.shape[1:])
    real_part = product[0, :, :, 0] - product[1, :, :, 1]
    imag_part = product[0, :, :, 1] + product[1, :, :, 0]
    return jnp.stack([real_part, imag_part], axis=2)


def mode_mix(values, matrix):
    return jnp.einsum("qrkp,qkn->qrnp", values, matrix, precision=lax.Precision.HIGHEST)


def rotate(summed, eigvec):
    real_in = summed[:, :, 0]
    imag_in = summed[:, :, 1]
    vec_real = eigvec[:, 0]
    vec_imag = eigvec[:, 1]
    real_out = mode_mix(real_in, vec_real) - mode_mix(imag_in, vec_imag)
    imag_out = mode_mix(real_in, vec_imag) + mode_mix(imag_in, vec_real)
    return jnp.stack([real_out, imag_out], axis=2)


def to_owners(all_points):
    return lax.all_to_all(all_points, "rp", split_axis=0, concat_axis=3, tiled=True)


def per_device(coupling, rp_coords, degeneracy, qpoints, eigvec):
    stacked = jnp.concatenate([rp_coords, degeneracy[None, :]], axis=0)
    lattice = lax.all_gather(stacked, "rp", axis=1, tiled=True)
    table = phases(qpoints, lattice[:3], lattice[3])
    rp_count = lax.axis_size("rp")
    re_count = lax.axis_size("re")
    local_rp, local_re, parts, mode_count, pair_count = coupling.shape
    q_local = eigvec.shape[0]
    pair_share = pair_count // re_count
    block_cols = mode_count * pair_share
    inner = block_cols // rp_count
    reordered = coupling.reshape(local_rp, local_re, parts, mode_count, re_count, pair_share)
    reordered = jnp.swapaxes(reordered, 3, 4)
    reordered = reordered.reshape(local_rp, local_re, parts, re_count, rp_count, inner)
    reordered = jnp.swapaxes(reordered, 3, 4)
    reordered = reordered.reshape(local_rp, local_re, parts, rp_count * re_count * inner)
    moved = lax.all_to_all(
        lax.all_to_all(reordered, "rp", split_axis=3, concat_axis=0, tiled=True),
        "re",
        split_axis=3,
        concat_axis=1,
        tiled=True,
    )
    all_points = combine(table, moved)
    summed = to_owners(all_points)
    summed = summed.reshape(q_local, summed.shape[1], parts, mode_count, pair_share)
    return rotate(summed, eigvec)


def column_of(angle):
    return [math.cos(2.0 * math.pi * (step - angle) / QGRID) for step in range(QGRID)]


def pick(turns, values):
    picked = jnp.full(turns.shape, values[0], jnp.float32)
    for step in range(1, QGRID):
        picked = jnp.where(turns == step, jnp.float32(values[step]), picked)
    return picked


def flip(index, bits):
    for bit in (1, 2, 4):
        if bits & bit:
            index = index + bit - 2 * bit * (index // bit % 2)
    return index


def place(index, gather):
    return 2 * (index // gather % 2) + index % 2


def rotation_kernel(
    n,
    planes,
    coupling,
    coords,
    degeneracy,
    eigvec,
    points_in,
    out,
    points,
    gathered,
    early,
    all_lattice,
    all_eigvec,
    table_rows,
    vectors,
    kept,
    leaving,
    arriving,
    turned,
    own_sem,
    small_send,
    small_recv,
    first_send,
    first_recv,
    middle_send,
    middle_recv,
    last_send,
    last_recv,
    above_sem,
):
    me = lax.axis_index("rp")
    plane = lax.axis_index("re")
    local_rp, modes, parts, pairs = coupling.shape
    share = pairs // planes
    lanes = gathered.shape[-1]
    q_local = eigvec.shape[-1]
    group = 4
    tile = parts * q_local
    half = group * tile
    pieces = 2
    width = group * local_rp * parts
    steps = (2, 3, 1, 0)
    sets = ((0, 4, 2), (1, 2, 4))
    near = (0, 1, 2, 3, 4, 5)

    barrier = pltpu.get_barrier_semaphore()

    def greet(semaphore, bits, level):
        pl.semaphore_signal(
            semaphore,
            inc=1,
            device_id={"rp": flip(me, bits), "re": level},
            device_id_type=MESH,
        )

    def local(source, target, index):
        return pltpu.make_async_copy(source, target, own_sem.at[index])

    def remote(source, target, send, recv, bits, step=0):
        return pltpu.make_async_remote_copy(
            src_ref=source,
            dst_ref=target,
            send_sem=send,
            recv_sem=recv,
            device_id={"rp": flip(me, bits), "re": flip(plane, step)},
            device_id_type=MESH,
        )

    def members(gather):
        return (gather + 1, gather, 1)

    def lattice_copies():
        return [
            remote(
                all_lattice.at[index, place(me, gather)],
                all_lattice.at[index, place(me, gather)],
                small_send.at[0],
                small_recv.at[0],
                bits,
            )
            for index, gather, _ in sets
            for turn, bits in enumerate(members(gather))
        ]

    def eigvec_copies():
        return [
            remote(
                all_eigvec.at[0],
                all_eigvec.at[turn],
                small_send.at[1],
                small_recv.at[1],
                bits,
            )
            for turn, bits in enumerate(near)
            if bits
        ]

    def bundle(held, send, recv):
        return remote(held, held, send, recv, 1)

    def lattice_all():
        held = all_lattice.at[:, pl.ds(0, group - 1)]
        return bundle(held, small_send.at[0], small_recv.at[0])

    def eigvec_all():
        return bundle(all_eigvec.at[pl.ds(1, len(near) - 1)], small_send.at[1], small_recv.at[1])

    def first_all(step, index):
        held = gathered.at[step, index, pl.ds(0, (group - 1) * local_rp)]
        return bundle(held, first_send.at[0], first_recv.at[step, index])

    def lattice_own():
        copies = []
        for index, gather, _ in sets:
            held = all_lattice.at[index, place(me, gather)]
            copies.append(local(coords, held.at[pl.ds(0, 3)], 2 * index))
            copies.append(local(degeneracy, held.at[pl.ds(3, 1)], 2 * index + 1))
        return copies

    def early_own():
        start = pl.multiple_of(flip(plane, steps[0]) * share, share)
        return local(coupling.at[:, :, :, pl.ds(start, share)], early, 16)

    eigvec_own = local(eigvec, all_eigvec.at[0], 4)
    points_own = local(points_in, points, 15)

    def piece(step, index, owner, gather):
        block = index * group + place(owner, gather)
        if step == steps[0]:
            return early.at[:, :, :, pl.ds(pl.multiple_of(block * lanes, lanes), lanes)]
        block = flip(plane, step) * 2 * group + block
        return coupling.at[:, :, :, pl.ds(pl.multiple_of(block * lanes, lanes), lanes)]

    def landing(step, index, gather):
        return gathered.at[step, index, pl.ds(place(me, gather) * local_rp, local_rp)]

    def first_copy(step, index, gather, bits):
        return remote(
            piece(step, index, flip(me, bits), gather),
            landing(step, index, gather),
            first_send.at[0],
            first_recv.at[step, index],
            bits,
        )

    def first_own(step, index, gather):
        return local(
            piece(step, index, me, gather),
            landing(step, index, gather),
            5 + 2 * step + index,
        )

    def send_first(step, turns=(0, 1, 2)):
        for turn in turns:
            for index, gather, _ in sets:
                first_copy(step, index, gather, members(gather)[turn]).start()
        if 2 in turns:
            for index, gather, _ in sets:
                first_own(step, index, gather).start()

    def middle_copy(step, index, other, side):
        rows = pl.ds(side * (half // pieces), half // pieces)
        return remote(
            leaving.at[step, index, rows],
            arriving.at[step, index, rows],
            middle_send.at[0],
            middle_recv.at[step, index, side],
            other,
        )

    def final_block(index, origin, gather):
        return index * group + place(origin, gather)

    def turned_at(step, index, side, core):
        return ((step * 2 + index) * 2 + side) * 2 + core

    def last_copy(step, index, gather, side, core):
        source = turned.at[turned_at(step, index, side, core)]
        target = out.at[plane * n + final_block(index, me, gather)]
        owner = flip(me, core) + gather * (side - me // gather % 2)
        return pltpu.make_async_remote_copy(
            src_ref=source,
            dst_ref=target,
            send_sem=last_send.at[0],
            recv_sem=last_recv.at[0],
            device_id={"rp": owner, "re": flip(plane, step)},
            device_id_type=MESH,
        )

    def last_all():
        count = n * planes - len(sets)
        return pltpu.make_async_remote_copy(
            src_ref=turned.at[pl.ds(0, count)],
            dst_ref=out.at[pl.ds(0, count)],
            send_sem=last_send.at[0],
            recv_sem=last_recv.at[0],
            device_id={"rp": flip(me, 1)},
            device_id_type=MESH,
        )

    def last_own(index, gather, side):
        return local(
            turned.at[turned_at(0, index, side, 0)],
            out.at[plane * n + final_block(index, me, gather)],
            13 + index,
        )

    def send_last(step, index, gather, side, core):
        if step or core:
            last_copy(step, index, gather, side, core).start()
            return
        same = me // gather % 2 == side

        @pl.when(same)
        def _():
            last_own(index, gather, side).start()

        @pl.when(jnp.logical_not(same))
        def _():
            last_copy(step, index, gather, side, core).start()

    early_own().start()
    for copy in lattice_own():
        copy.start()
    points_own.start()
    eigvec_own.start()
    for bits in near[1:]:
        greet(barrier, bits, plane)
    for ahead in range(1, planes):

        @pl.when(plane + ahead < planes)
        def _():
            for bits in near:
                greet(barrier, bits, plane + ahead)

    for copy in lattice_own():
        copy.wait()
    early_own().wait()
    pl.semaphore_wait(barrier, len(near) - 1 + len(near) * plane)
    for copy in lattice_copies():
        copy.start()
    send_first(steps[0])
    for behind in range(1, planes):

        @pl.when(plane >= behind)
        def _():
            greet(above_sem, 0, plane - behind)
    eigvec_own.wait()
    for copy in eigvec_copies():
        copy.start()
    send_first(steps[1])

    points_own.wait()
    lattice_all().wait_recv()

    columns = lax.broadcasted_iota(jnp.int32, (group * local_rp, width), 1)
    repeat = columns // parts == lax.broadcasted_iota(jnp.int32, (group * local_rp, width), 0)
    repeat = repeat.astype(jnp.bfloat16)

    def twice(index):
        row = jnp.concatenate([all_lattice[index, slot] for slot in range(group)], axis=1)
        row = row.astype(jnp.float32).astype(jnp.bfloat16)
        return jnp.dot(row, repeat, preferred_element_type=jnp.float32)

    q_count = n * q_local
    real_part = lax.broadcasted_iota(jnp.int32, (q_count, width), 1) % parts == 0
    tables = []
    for index, gather, other in sets:
        lattice = twice(index)
        turns = lax.dot_general(
            points[...].astype(jnp.float32).astype(jnp.bfloat16),
            lattice[:3].astype(jnp.bfloat16),
            (((0,), (0,)), ((), ())),
            preferred_element_type=jnp.float32,
        )
        turns = turns.astype(jnp.int32) & (QGRID - 1)
        weights = 1.0 / lattice[3:]
        cos = pick(turns, column_of(0.0)) * weights
        sin = pick(turns, column_of(QGRID / 4)) * weights
        to_real = jnp.where(real_part, cos, -sin)
        to_imag = jnp.where(real_part, sin, cos)
        mine = me // other % 2
        for owner in range(n):
            across = owner // other % 2
            apart = across + mine - 2 * across * mine
            row = pl.multiple_of((1 - apart) * half + place(owner, gather) * tile, tile)
            rows = slice(owner * q_local, (owner + 1) * q_local)
            table_rows[index, pl.ds(row, q_local), :] = to_real[rows]
            table_rows[index, pl.ds(row + q_local, q_local), :] = to_imag[rows]

    def gather_step(step):
        for index, gather, other in sets:
            first_own(step, index, gather).wait()
            first_all(step, index).wait_recv()
            table = table_rows[index].astype(jnp.bfloat16)
            for mode in range(modes):
                product = jnp.dot(
                    table,
                    gathered[step, index, :, mode].reshape(width, lanes),
                    preferred_element_type=jnp.float32,
                )
                at = slice(mode * lanes, (mode + 1) * lanes)
                leaving[step, index, :, at] = product[:half].astype(jnp.bfloat16)
                kept[step, index, :, at] = product[half:]
            for side in range(pieces):
                middle_copy(step, index, other, side).start()

    def rotate_step(step):
        for side in range(pieces):
            for index, gather, other in sets:
                middle_copy(step, index, other, side).wait_recv()
                apart = (me // gather + side) % 2
                for core in (1, 0):
                    start = pl.multiple_of((2 * side + (me + core) % 2) * tile, tile)
                    rows = pl.ds(start, tile)
                    owner = apart * gather + core
                    real_in = []
                    imag_in = []
                    for k in range(modes):
                        at = slice(k * lanes, (k + 1) * lanes)
                        total = kept[step, index, rows, at] + arriving[
                            step, index, rows, at
                        ].astype(jnp.float32)
                        real_in.append(total[:q_local])
                        imag_in.append(total[q_local:])
                    for mode in range(modes):
                        real_out = jnp.zeros((q_local, lanes), jnp.float32)
                        imag_out = jnp.zeros((q_local, lanes), jnp.float32)
                        for k in range(modes):
                            vec_real = vectors[owner, (k * modes + mode) * parts]
                            vec_imag = vectors[owner, (k * modes + mode) * parts + 1]
                            real_out += real_in[k] * vec_real - imag_in[k] * vec_imag
                            imag_out += real_in[k] * vec_imag + imag_in[k] * vec_real
                        turned[turned_at(step, index, side, core), mode] = jnp.concatenate(
                            [real_out, imag_out], axis=0
                        ).astype(jnp.bfloat16)
                    send_last(step, index, gather, side, core)

    gather_step(steps[0])
    eigvec_all().wait_recv()
    for turn in range(len(near)):
        flat = all_eigvec[turn].reshape(modes * modes * parts, q_local).T
        for entry in range(modes * modes * parts):
            vectors[turn, entry] = jnp.broadcast_to(flat[:, entry : entry + 1], (q_local, lanes))
    send_first(steps[2])
    gather_step(steps[1])

    @pl.when(plane < planes - 1)
    def _():
        pl.semaphore_wait(above_sem, planes - 1 - plane)

    rotate_step(steps[0])
    send_first(steps[3])
    gather_step(steps[2])
    rotate_step(steps[1])
    gather_step(steps[3])
    rotate_step(steps[2])
    rotate_step(steps[3])

    lattice_all().wait_send()
    eigvec_all().wait_send()
    everything = gathered.at[:, :, pl.ds(0, (group - 1) * local_rp)]
    bundle(everything, first_send.at[0], first_recv.at[0, 0]).wait_send()
    bundle(leaving, middle_send.at[0], middle_recv.at[0, 0, 0]).wait_send()
    for index, gather, _ in sets:
        last_own(index, gather, me // gather % 2).wait()
    last_all().wait_recv()
    last_all().wait_send()


def spread_kernel(planes, held, out, rows_of, sems):
    _, modes, tile, lanes = held.shape
    blocks = held.shape[0] // planes
    q_local = tile // 2
    per_plane = modes * blocks * 2
    per_q = planes * per_plane

    def copies(source):
        return [
            pltpu.make_async_copy(
                rows_of.at[pl.ds(q * per_q + source * per_plane, per_plane)],
                out.at[pl.ds(q * per_q + source * per_plane, per_plane)],
                sems.at[source, q],
            )
            for q in range(q_local)
        ]

    for source in range(planes):
        for mode in range(modes):
            for block in range(blocks):
                values = held[source * blocks + block, mode].astype(jnp.float32)
                row = source * per_plane + (mode * blocks + block) * 2
                rows_of[pl.ds(row, q_local, stride=per_q), :] = values[:q_local]
                rows_of[pl.ds(row + 1, q_local, stride=per_q), :] = values[q_local:]
        for copy in copies(source):
            copy.start()
    for source in range(planes):
        for copy in copies(source):
            copy.wait()


def in_hbm(value):
    return pltpu.with_memory_space_constraint(value, pltpu.HBM)


def exchanged(coupling, rp_coords, degeneracy, qpoints, eigvec):
    n = lax.axis_size("rp")
    planes = lax.axis_size("re")
    local_rp, local_re, parts, modes, pairs = coupling.shape
    q_local = eigvec.shape[0]
    lanes = pairs // planes // n
    group = n // 2
    tile = parts * q_local
    half = group * tile
    width = group * local_rp * parts
    entries = parts * modes * modes
    near = 6
    gathered = pl.pallas_call(
        functools.partial(rotation_kernel, n, planes),
        out_shape=jax.ShapeDtypeStruct((planes * n, modes, tile, lanes), jnp.bfloat16),
        in_specs=[
            pl.BlockSpec(memory_space=pltpu.HBM),
            pl.BlockSpec(memory_space=pltpu.HBM),
            pl.BlockSpec(memory_space=pltpu.HBM),
            pl.BlockSpec(memory_space=pltpu.HBM),
            pl.BlockSpec(memory_space=pltpu.HBM),
        ],
        out_specs=pl.BlockSpec(memory_space=pl.ANY),
        scratch_shapes=[
            pltpu.VMEM(qpoints.shape, jnp.int32),
            pltpu.VMEM((planes, 2, group * local_rp, modes, parts, lanes), jnp.bfloat16),
            pltpu.VMEM((local_rp, modes, parts, pairs // planes), jnp.bfloat16),
            pltpu.VMEM((2, group, rp_coords.shape[0] + 1, local_rp), jnp.int32),
            pltpu.VMEM((near, modes * modes, parts, q_local), jnp.float32),
            pltpu.VMEM((2, 2 * half, width), jnp.float32),
            pltpu.VMEM((near, entries, q_local, lanes), jnp.float32),
            pltpu.VMEM((planes, 2, half, modes * lanes), jnp.float32),
            pltpu.VMEM((planes, 2, half, modes * lanes), jnp.bfloat16),
            pltpu.VMEM((planes, 2, half, modes * lanes), jnp.bfloat16),
            pltpu.VMEM((planes * n, modes, tile, lanes), jnp.bfloat16),
            pltpu.SemaphoreType.DMA((17,)),
            pltpu.SemaphoreType.DMA((2,)),
            pltpu.SemaphoreType.DMA((2,)),
            pltpu.SemaphoreType.DMA((1,)),
            pltpu.SemaphoreType.DMA((planes, 2)),
            pltpu.SemaphoreType.DMA((1,)),
            pltpu.SemaphoreType.DMA((planes, 2, 2)),
            pltpu.SemaphoreType.DMA((1,)),
            pltpu.SemaphoreType.DMA((1,)),
            pltpu.SemaphoreType.REGULAR,
        ],
        compiler_params=pltpu.CompilerParams(
            collective_id=0, has_side_effects=True, vmem_limit_bytes=24 * 2**20
        ),
    )(
        in_hbm(jnp.swapaxes(coupling[:, 0], 1, 2)),
        in_hbm(rp_coords),
        in_hbm(degeneracy[None, :]),
        in_hbm(jnp.transpose(eigvec, (2, 3, 1, 0)).reshape(modes * modes, parts, q_local)),
        in_hbm(qpoints),
    )
    rows = q_local * planes * modes * n * parts
    spread = pl.pallas_call(
        functools.partial(spread_kernel, planes),
        out_shape=jax.ShapeDtypeStruct((rows, lanes), jnp.float32),
        in_specs=[pl.BlockSpec(memory_space=pltpu.VMEM)],
        out_specs=pl.BlockSpec(memory_space=pl.ANY),
        scratch_shapes=[
            pltpu.VMEM((rows, lanes), jnp.float32),
            pltpu.SemaphoreType.DMA((planes, q_local)),
        ],
        compiler_params=pltpu.CompilerParams(vmem_limit_bytes=24 * 2**20),
    )(gathered)
    spread = spread.reshape(q_local, planes, modes, n, parts, lanes)
    spread = jnp.transpose(spread, (0, 1, 4, 2, 3, 5))
    return spread.reshape(q_local, planes, parts, modes, n * lanes)


def fits(n, planes, coupling, eigvec):
    local_rp, local_re, parts, modes, pairs = coupling.shape
    return (
        local_re == 1
        and n == 8
        and planes == 4
        and local_rp * n == 128
        and parts * modes * modes <= 128
        and pairs // planes // n == 128
        and eigvec.shape[0] == 8
        and modes <= 8
    )


def either(coupling, rp_coords, degeneracy, qpoints, eigvec):
    if fits(lax.axis_size("rp"), lax.axis_size("re"), coupling, eigvec):
        return exchanged(coupling, rp_coords, degeneracy, qpoints, eigvec)
    return per_device(coupling, rp_coords, degeneracy, qpoints, eigvec)


def solution(mesh):
    return jax.shard_map(
        either,
        mesh=mesh,
        in_specs=(
            P("rp", "re", None, None, None),
            P(None, "rp"),
            P("rp"),
            P(),
            P("rp", None, None, None),
        ),
        out_specs=P("rp", None, None, None, "re"),
        check_vma=False,
    )
```

time: 37.3 us -> 33.5 us (0.90)
  the two profiles are of different devices: /device:TPU:0 before, /device:TPU:3 now
where the time goes in v3:
time: 33.5 us; the launch traced here: 33.4 us
  Pallas kernels  33.4 us (100%)
    pallas_call x1, Pallas kernels, exchanged(): pl.pallas_call(functools.partial(rotation_kernel, n, planes), out_shape=j...  31.4 us
    pallas_call x1, Pallas kernels, exchanged(): pl.pallas_call(functools.partial(spread_kernel, planes), out_shape=jax.Sh...  1.94 us

profile of v3, /device:TPU:3, one launch (start us, length us, event | category | flops | bytes accessed | tf_op | source)
XLA Modules:
  0.0 33.4 jit_solution(7889897130071147563)
XLA Ops:
  0.0 31.4 %shard_map.55.held = bf16[32,6,16,128]{3,2,1,0:T(8,128)(2,1)S(1)} custom-call(bf16[16,6,2,4096]{3,2,1,0:T(2,128)(2,1)} %bitcast.12, s32[3,16]{1,0:T(4,128)} %coords.1, s32[1,16]{1,0:T(1,128)} %bitcast.14, f32[36,2,8]{2,1,0:T(2,128)} %bitcast.13, s32[3,64]{1,0:T(4,128)} %points_in.1), custom_call_target="tpu_custom_call" | custom-call | tf_op jit(solution)/shard_map/pallas_call | solution.py:526
  31.4 1.9 %shard_map.56 = f32[3072,128]{1,0:T(8,128)} custom-call(bf16[32,6,16,128]{3,2,1,0:T(8,128)(2,1)S(1)} %shard_map.55.held), custom_call_target="tpu_custom_call" | custom-call | tf_op jit(solution)/shard_map/pallas_call | solution.py:571

commit v4 on v3

--- a/solution.py
+++ b/solution.py
@@ -118,6 +118,7 @@
     gathered,
     early,
     all_lattice,
+    own_eigvec,
     all_eigvec,
     table_rows,
     vectors,
@@ -229,7 +230,7 @@
         start = pl.multiple_of(flip(plane, steps[0]) * share, share)
         return local(coupling.at[:, :, :, pl.ds(start, share)], early, 16)
 
-    eigvec_own = local(eigvec, all_eigvec.at[0], 4)
+    eigvec_own = local(eigvec, own_eigvec, 4)
     points_own = local(points_in, points, 15)
 
     def piece(step, index, owner, gather):
@@ -354,6 +355,8 @@
         def _():
             greet(above_sem, 0, plane - behind)
     eigvec_own.wait()
+    entries = modes * modes * parts
+    all_eigvec[0, :, :entries] = own_eigvec[...].reshape(entries, q_local).T
     for copy in eigvec_copies():
         copy.start()
     send_first(steps[1])
@@ -447,8 +450,8 @@
     gather_step(steps[0])
     eigvec_all().wait_recv()
     for turn in range(len(near)):
-        flat = all_eigvec[turn].reshape(modes * modes * parts, q_local).T
-        for entry in range(modes * modes * parts):
+        flat = all_eigvec[turn]
+        for entry in range(entries):
             vectors[turn, entry] = jnp.broadcast_to(flat[:, entry : entry + 1], (q_local, lanes))
     send_first(steps[2])
     gather_step(steps[1])
@@ -539,7 +542,8 @@
             pltpu.VMEM((planes, 2, group * local_rp, modes, parts, lanes), jnp.bfloat16),
             pltpu.VMEM((local_rp, modes, parts, pairs // planes), jnp.bfloat16),
             pltpu.VMEM((2, group, rp_coords.shape[0] + 1, local_rp), jnp.int32),
-            pltpu.VMEM((near, modes * modes, parts, q_local), jnp.float32),
+            pltpu.VMEM((modes * modes, parts, q_local), jnp.float32),
+            pltpu.VMEM((near, q_local, lanes), jnp.float32),
             pltpu.VMEM((2, 2 * half, width), jnp.float32),
             pltpu.VMEM((near, entries, q_local, lanes), jnp.float32),
             pltpu.VMEM((planes, 2, half, modes * lanes), jnp.float32),

time: 33.5 us -> 32.1 us (0.958)
  Pallas kernels: 33.4 us -> 32 us
    pallas_call x1, Pallas kernels: 31.4 us -> 30 us  [exchanged(): pl.pallas_call(functools.partial(rotation_kernel, n, planes), out_shape=j...]
where the time goes in v4:
time: 32.1 us; the launch traced here: 32 us
  Pallas kernels  32 us (100%)
    pallas_call x1, Pallas kernels, exchanged(): pl.pallas_call(functools.partial(rotation_kernel, n, planes), out_shape=j...  30 us
    pallas_call x1, Pallas kernels, exchanged(): pl.pallas_call(functools.partial(spread_kernel, planes), out_shape=jax.Sh...  1.94 us

profile of v4, /device:TPU:3, one launch (start us, length us, event | category | flops | bytes accessed | tf_op | source)
XLA Modules:
  0.0 32.0 jit_solution(4554686485525809931)
XLA Ops:
  0.0 30.0 %shard_map.55.held = bf16[32,6,16,128]{3,2,1,0:T(8,128)(2,1)S(1)} custom-call(bf16[16,6,2,4096]{3,2,1,0:T(2,128)(2,1)} %bitcast.12, s32[3,16]{1,0:T(4,128)} %coords.1, s32[1,16]{1,0:T(1,128)} %bitcast.14, f32[36,2,8]{2,1,0:T(2,128)} %bitcast.13, s32[3,64]{1,0:T(4,128)} %points_in.1), custom_call_target="tpu_custom_call" | custom-call | tf_op jit(solution)/shard_map/pallas_call | solution.py:529
  30.0 1.9 %shard_map.56 = f32[3072,128]{1,0:T(8,128)} custom-call(bf16[32,6,16,128]{3,2,1,0:T(8,128)(2,1)S(1)} %shard_map.55.held), custom_call_target="tpu_custom_call" | custom-call | tf_op jit(solution)/shard_map/pallas_call | solution.py:575

commit v5 on v4

--- a/solution.py
+++ b/solution.py
@@ -103,6 +103,16 @@
 
 def place(index, gather):
     return 2 * (index // gather % 2) + index % 2
+
+
+ORDER = ((2, 3, 1, 0), (3, 2, 0, 1), (0, 1, 3, 2), (0, 1, 2, 3))
+
+
+def aim(plane, turn):
+    target = ORDER[0][turn]
+    for level in range(1, len(ORDER)):
+        target = jnp.where(plane == level, ORDER[level][turn], target)
+    return target
 
 
 def rotation_kernel(
@@ -146,9 +156,10 @@
     group = 4
     tile = parts * q_local
     half = group * tile
-    pieces = 2
+    pieces = 4
     width = group * local_rp * parts
-    steps = (2, 3, 1, 0)
+    steps = tuple(range(planes))
+    aims = [aim(plane, turn) for turn in steps]
     sets = ((0, 4, 2), (1, 2, 4))
     near = (0, 1, 2, 3, 4, 5)
 
@@ -227,7 +238,7 @@
         return copies
 
     def early_own():
-        start = pl.multiple_of(flip(plane, steps[0]) * share, share)
+        start = pl.multiple_of(aims[0] * share, share)
         return local(coupling.at[:, :, :, pl.ds(start, share)], early, 16)
 
     eigvec_own = local(eigvec, own_eigvec, 4)
@@ -237,7 +248,7 @@
         block = index * group + place(owner, gather)
         if step == steps[0]:
             return early.at[:, :, :, pl.ds(pl.multiple_of(block * lanes, lanes), lanes)]
-        block = flip(plane, step) * 2 * group + block
+        block = aims[step] * 2 * group + block
         return coupling.at[:, :, :, pl.ds(pl.multiple_of(block * lanes, lanes), lanes)]
 
     def landing(step, index, gather):
@@ -286,13 +297,13 @@
     def last_copy(step, index, gather, side, core):
         source = turned.at[turned_at(step, index, side, core)]
         target = out.at[plane * n + final_block(index, me, gather)]
-        owner = flip(me, core) + gather * (side - me // gather % 2)
+        owner = me + core - me % 2 + gather * (side - me // gather % 2)
         return pltpu.make_async_remote_copy(
             src_ref=source,
             dst_ref=target,
             send_sem=last_send.at[0],
             recv_sem=last_recv.at[0],
-            device_id={"rp": owner, "re": flip(plane, step)},
+            device_id={"rp": owner, "re": aims[step]},
             device_id_type=MESH,
         )
 
@@ -309,16 +320,16 @@
 
     def last_own(index, gather, side):
         return local(
-            turned.at[turned_at(0, index, side, 0)],
+            turned.at[turned_at(planes - 1, index, side, me % 2)],
             out.at[plane * n + final_block(index, me, gather)],
             13 + index,
         )
 
     def send_last(step, index, gather, side, core):
-        if step or core:
+        if step < planes - 1:
             last_copy(step, index, gather, side, core).start()
             return
-        same = me // gather % 2 == side
+        same = jnp.logical_and(me // gather % 2 == side, me % 2 == core)
 
         @pl.when(same)
         def _():
@@ -417,14 +428,15 @@
                 middle_copy(step, index, other, side).start()
 
     def rotate_step(step):
-        for side in range(pieces):
+        for piece_at in range(pieces):
             for index, gather, other in sets:
-                middle_copy(step, index, other, side).wait_recv()
+                side = piece_at // 2
+                middle_copy(step, index, other, piece_at).wait_recv()
                 apart = (me // gather + side) % 2
-                for core in (1, 0):
-                    start = pl.multiple_of((2 * side + (me + core) % 2) * tile, tile)
+                for core in (0,):
+                    start = pl.multiple_of(piece_at * tile, tile)
                     rows = pl.ds(start, tile)
-                    owner = apart * gather + core
+                    owner = apart * gather + (me + piece_at) % 2
                     real_in = []
                     imag_in = []
                     for k in range(modes):
@@ -442,10 +454,10 @@
                             vec_imag = vectors[owner, (k * modes + mode) * parts + 1]
                             real_out += real_in[k] * vec_real - imag_in[k] * vec_imag
                             imag_out += real_in[k] * vec_imag + imag_in[k] * vec_real
-                        turned[turned_at(step, index, side, core), mode] = jnp.concatenate(
+                        turned[turned_at(step, index, side, piece_at % 2), mode] = jnp.concatenate(
                             [real_out, imag_out], axis=0
                         ).astype(jnp.bfloat16)
-                    send_last(step, index, gather, side, core)
+                    send_last(step, index, gather, side, piece_at % 2)
 
     gather_step(steps[0])
     eigvec_all().wait_recv()
@@ -484,17 +496,12 @@
     blocks = held.shape[0] // planes
     q_local = tile // 2
     per_plane = modes * blocks * 2
-    per_q = planes * per_plane
-
-    def copies(source):
-        return [
-            pltpu.make_async_copy(
-                rows_of.at[pl.ds(q * per_q + source * per_plane, per_plane)],
-                out.at[pl.ds(q * per_q + source * per_plane, per_plane)],
-                sems.at[source, q],
-            )
-            for q in range(q_local)
-        ]
+    per_q = rows_of.shape[0] // q_local
+    by_q = rows_of.reshape(q_local, per_q, lanes)
+
+    def spread(source):
+        rows = pl.ds(source * per_plane, per_plane)
+        return pltpu.make_async_copy(by_q.at[:, rows], out.at[:, rows], sems.at[source])
 
     for source in range(planes):
         for mode in range(modes):
@@ -503,11 +510,9 @@
                 row = source * per_plane + (mode * blocks + block) * 2
                 rows_of[pl.ds(row, q_local, stride=per_q), :] = values[:q_local]
                 rows_of[pl.ds(row + 1, q_local, stride=per_q), :] = values[q_local:]
-        for copy in copies(source):
-            copy.start()
+        spread(source).start()
     for source in range(planes):
-        for copy in copies(source):
-            copy.wait()
+        spread(source).wait()
 
 
 def in_hbm(value):
@@ -556,7 +561,7 @@
             pltpu.SemaphoreType.DMA((1,)),
             pltpu.SemaphoreType.DMA((planes, 2)),
             pltpu.SemaphoreType.DMA((1,)),
-            pltpu.SemaphoreType.DMA((planes, 2, 2)),
+            pltpu.SemaphoreType.DMA((planes, 2, 4)),
             pltpu.SemaphoreType.DMA((1,)),
             pltpu.SemaphoreType.DMA((1,)),
             pltpu.SemaphoreType.REGULAR,
@@ -571,15 +576,15 @@
         in_hbm(jnp.transpose(eigvec, (2, 3, 1, 0)).reshape(modes * modes, parts, q_local)),
         in_hbm(qpoints),
     )
-    rows = q_local * planes * modes * n * parts
+    rows = planes * modes * n * parts
     spread = pl.pallas_call(
         functools.partial(spread_kernel, planes),
-        out_shape=jax.ShapeDtypeStruct((rows, lanes), jnp.float32),
+        out_shape=jax.ShapeDtypeStruct((q_local, rows, lanes), jnp.float32),
         in_specs=[pl.BlockSpec(memory_space=pltpu.VMEM)],
         out_specs=pl.BlockSpec(memory_space=pl.ANY),
         scratch_shapes=[
-            pltpu.VMEM((rows, lanes), jnp.float32),
-            pltpu.SemaphoreType.DMA((planes, q_local)),
+            pltpu.VMEM((q_local * (rows + 8), lanes), jnp.float32),
+            pltpu.SemaphoreType.DMA((planes,)),
         ],
         compiler_params=pltpu.CompilerParams(vmem_limit_bytes=24 * 2**20),
     )(gathered)

time: 32.1 us -> 29.9 us (0.931)
  the two profiles are of different devices: /device:TPU:3 before, /device:TPU:0 now
where the time goes in v5:
time: 29.9 us; the launch traced here: 29.4 us
  Pallas kernels  29.4 us (98%)
    pallas_call x1, Pallas kernels, exchanged(): pl.pallas_call(functools.partial(rotation_kernel, n, planes), out_shape=j...  28.2 us
    pallas_call x1, Pallas kernels, exchanged(): pl.pallas_call(functools.partial(spread_kernel, planes), out_shape=jax.Sh...  1.23 us

profile of v5, /device:TPU:0, one launch (start us, length us, event | category | flops | bytes accessed | tf_op | source)
XLA Modules:
  0.0 29.4 jit_solution(9257932287785755752)
XLA Ops:
  0.0 28.2 %shard_map.55.held = bf16[32,6,16,128]{3,2,1,0:T(8,128)(2,1)S(1)} custom-call(bf16[16,6,2,4096]{3,2,1,0:T(2,128)(2,1)} %bitcast.12, s32[3,16]{1,0:T(4,128)} %coords.1, s32[1,16]{1,0:T(1,128)} %bitcast.14, f32[36,2,8]{2,1,0:T(2,128)} %bitcast.13, s32[3,64]{1,0:T(4,128)} %points_in.1), custom_call_target="tpu_custom_call" | custom-call | tf_op jit(solution)/shard_map/pallas_call | solution.py:534
  28.2 1.2 %shard_map.56 = f32[8,384,128]{2,1,0:T(8,128)} custom-call(bf16[32,6,16,128]{3,2,1,0:T(8,128)(2,1)S(1)} %shard_map.55.held), custom_call_target="tpu_custom_call" | custom-call | tf_op jit(solution)/shard_map/pallas_call | solution.py:580

commit v6 on v5

--- a/solution.py
+++ b/solution.py
@@ -339,11 +339,6 @@
         def _():
             last_copy(step, index, gather, side, core).start()
 
-    early_own().start()
-    for copy in lattice_own():
-        copy.start()
-    points_own.start()
-    eigvec_own.start()
     for bits in near[1:]:
         greet(barrier, bits, plane)
     for ahead in range(1, planes):
@@ -353,6 +348,11 @@
             for bits in near:
                 greet(barrier, bits, plane + ahead)
 
+    for copy in lattice_own():
+        copy.start()
+    early_own().start()
+    points_own.start()
+    eigvec_own.start()
     for copy in lattice_own():
         copy.wait()
     early_own().wait()
@@ -360,17 +360,17 @@
     for copy in lattice_copies():
         copy.start()
     send_first(steps[0])
-    for behind in range(1, planes):
-
-        @pl.when(plane >= behind)
-        def _():
-            greet(above_sem, 0, plane - behind)
     eigvec_own.wait()
     entries = modes * modes * parts
     all_eigvec[0, :, :entries] = own_eigvec[...].reshape(entries, q_local).T
     for copy in eigvec_copies():
         copy.start()
     send_first(steps[1])
+    for behind in range(1, planes):
+
+        @pl.when(plane >= behind)
+        def _():
+            greet(above_sem, 0, plane - behind)
 
     points_own.wait()
     lattice_all().wait_recv()
@@ -460,20 +460,20 @@
                     send_last(step, index, gather, side, piece_at % 2)
 
     gather_step(steps[0])
+    send_first(steps[2])
     eigvec_all().wait_recv()
     for turn in range(len(near)):
         flat = all_eigvec[turn]
         for entry in range(entries):
             vectors[turn, entry] = jnp.broadcast_to(flat[:, entry : entry + 1], (q_local, lanes))
-    send_first(steps[2])
     gather_step(steps[1])
+    send_first(steps[3])
 
     @pl.when(plane < planes - 1)
     def _():
         pl.semaphore_wait(above_sem, planes - 1 - plane)
 
     rotate_step(steps[0])
-    send_first(steps[3])
     gather_step(steps[2])
     rotate_step(steps[1])
     gather_step(steps[3])

time: 29.9 us -> 29.9 us (level)
  no operation moved by 1% of the time
where the time goes in v6:
time: 29.9 us; the launch traced here: 29.6 us
  Pallas kernels  29.6 us (99%)
    pallas_call x1, Pallas kernels, exchanged(): pl.pallas_call(functools.partial(rotation_kernel, n, planes), out_shape=j...  28.4 us
    pallas_call x1, Pallas kernels, exchanged(): pl.pallas_call(functools.partial(spread_kernel, planes), out_shape=jax.Sh...  1.23 us

profile of v6, /device:TPU:0, one launch (start us, length us, event | category | flops | bytes accessed | tf_op | source)
XLA Modules:
  0.0 29.6 jit_solution(8607376737983812700)
XLA Ops:
  0.0 28.4 %shard_map.55.held = bf16[32,6,16,128]{3,2,1,0:T(8,128)(2,1)S(1)} custom-call(bf16[16,6,2,4096]{3,2,1,0:T(2,128)(2,1)} %bitcast.12, s32[3,16]{1,0:T(4,128)} %coords.1, s32[1,16]{1,0:T(1,128)} %bitcast.14, f32[36,2,8]{2,1,0:T(2,128)} %bitcast.13, s32[3,64]{1,0:T(4,128)} %points_in.1), custom_call_target="tpu_custom_call" | custom-call | tf_op jit(solution)/shard_map/pallas_call | solution.py:534
  28.4 1.2 %shard_map.56 = f32[8,384,128]{2,1,0:T(8,128)} custom-call(bf16[32,6,16,128]{3,2,1,0:T(8,128)(2,1)S(1)} %shard_map.55.held), custom_call_target="tpu_custom_call" | custom-call | tf_op jit(solution)/shard_map/pallas_call | solution.py:580
